TPU v7x, 128 devices: a whole 4x4x4 slice. The times are simulated.
128 devices in a mesh: row: 8 (over y_hi, z), col: 16 (over x, y_lo, core).
Axes of the slice: x: 4, y: 4 (y_hi: 2, y_lo: 2; y = y_hi * 2 + y_lo), z: 4, core: 2. Of those that a mesh axis runs over, the one named last changes fastest.
Arguments:
- response_coeffs: float32 [3, 8192, 1024], P(None, ('row', 'col')), may hold values from -6 to 6
- occupied_coeffs: float32 [8192, 1024], P(('row', 'col')), may hold values from -0.1875 to 0.1875
Outputs:
- density: float32 [3, 8192, 8192], P(None, 'row', 'col')
All inputs are finite; a program needn't handle non-finite values.
Results may differ from a plain program's by a relative error of at most 0.0003.
Values sent between devices are 32-bit elements; how exact they have to be, the bound alone decides.
A program may use at most 128 MiB of HBM per device.

v0:
```python
import jax
import jax.numpy as jnp
from jax import lax
from jax.sharding import PartitionSpec as P

SLICE_PAIRS = ((0, 0), (0, 1), (1, 0))


def broadcast(value, axis, source):
    kept = jnp.where(lax.axis_index(axis) == source, value, 0).astype(value.dtype)
    return lax.psum(kept, axis)


def split_slices(values):
    leading = lax.optimization_barrier(values.astype(jnp.bfloat16))
    remainder = values - leading.astype(jnp.float32)
    trailing = lax.optimization_barrier(remainder.astype(jnp.bfloat16))
    return [leading, trailing]


def contribute(row_slices, column_slices, perturbations):
    accumulated = jnp.zeros(
        (perturbations, row_slices[0].shape[1], column_slices[0].shape[1]), jnp.float32
    )
    for left_index, right_index in SLICE_PAIRS:
        forward_term = jnp.einsum(
            "kro,co->krc",
            row_slices[left_index][:perturbations],
            column_slices[right_index][perturbations],
            preferred_element_type=jnp.float32,
        )
        mirror_term = jnp.einsum(
            "ro,kco->krc",
            row_slices[right_index][perturbations],
            column_slices[left_index][:perturbations],
            preferred_element_type=jnp.float32,
        )
        accumulated = accumulated + forward_term + mirror_term
    return accumulated


def shards(response_coeffs, occupied_coeffs):
    perturbations = response_coeffs.shape[0]
    stacked = jnp.concatenate([response_coeffs, occupied_coeffs[None]], axis=0)
    col_index = lax.axis_index("col")
    row_panel = lax.all_gather(stacked, "col", axis=1, tiled=True)
    half_rows = row_panel.shape[1] // 2
    own_half = lax.dynamic_slice_in_dim(row_panel, col_index % 2 * half_rows, half_rows, 1)
    column_panel = broadcast(own_half, "row", col_index // 2)
    density = contribute(split_slices(row_panel), split_slices(column_panel), perturbations)
    return density


def solution(mesh):
    return jax.shard_map(
        shards,
        mesh=mesh,
        in_specs=(P(None, ("row", "col"), None), P(("row", "col"), None)),
        out_specs=P(None, "row", "col"),
        check_vma=False,
    )
```

profile of v0, /device:TPU:1, one launch (start us, length us, event | category | flops | bytes accessed | tf_op | source)
XLA Modules:
  0.0 361.2 jit_solution(1945731837348868768)
XLA Ops:
  6.5 0.0 all-gather.2.cloned.1.call-start
  6.5 2.3 pad_maximum_fusion
  8.8 0.0 all-gather.2.cloned.1.call-update
  8.9 0.0 all-reduce.2.cloned.1.call-start
  8.9 95.2 %all-gather.2.cloned.1.call-done = f32[4,1024,1024]{2,1,0:T(8,128)} async-done(((f32[4,64,1024]{2,1,0:T(8,128)}), f32[4,1024,1024]{2,1,0:T(8,128)}) %all-gather.2.cloned.1.call-update) | async-done | bytes 16777232 | tf_op jit(solution)/shard_map/all_gather | solution.py:46
  104.2 8.5 %dynamic-slice_select_fusion = f32[4,512,1024]{2,1,0:T(8,128)} fusion(f32[4,1024,1024]{2,1,0:T(8,128)} %all-gather.2.cloned.1.call-done, s32[]{:T(128)S(6)} %select_n.25, pred[]{:T(512)S(6)} %eq.5), kind=kLoop, calls=%fused_computation.2 | loop fusion | flops 2097152 | bytes 16777220 | tf_op jit(solution)/shard_map/jit(_where)/select_n | solution.py:10
  112.7 0.0 all-reduce.2.cloned.1.call-update
  112.7 6.6 %convert_element_type.20 = bf16[4,1024,1024]{2,1,0:T(8,128)(2,1)S(1)} convert(f32[4,1024,1024]{2,1,0:T(8,128)} %all-gather.2.cloned.1.call-done) | non-fusion elementwise | flops 4194304 | bytes 25165824 | tf_op jit(solution)/shard_map/convert_element_type | solution.py:15
  119.3 0.0 copy-start
  119.3 3.5 copy-done
  122.8 10.2 %subtract_convert_fusion = bf16[4,1024,1024]{2,1,0:T(8,128)(2,1)} fusion(f32[4,1024,1024]{2,1,0:T(8,128)} %all-gather.2.cloned.1.call-done, bf16[4,1024,1024]{2,1,0:T(8,128)(2,1)S(1)} %convert_element_type.20), kind=kLoop, calls=%fused_computation | loop fusion | flops 12582912 | bytes 33554432 | tf_op jit(solution)/shard_map/convert_element_type | solution.py:17
  133.0 166.2 %all-reduce.2.cloned.1.call-done = f32[4,512,1024]{2,1,0:T(8,128)} async-done(((f32[4,512,1024]{2,1,0:T(8,128)}), f32[4,512,1024]{2,1,0:T(8,128)}) %all-reduce.2.cloned.1.call-update) | async-done | bytes 8388624 | tf_op jit(solution)/shard_map/psum | solution.py:11
  299.1 4.2 %convert_element_type.21 = bf16[4,512,1024]{2,1,0:T(8,128)(2,1)S(1)} convert(f32[4,512,1024]{2,1,0:T(8,128)} %all-reduce.2.cloned.1.call-done) | non-fusion elementwise | flops 2097152 | bytes 12582912 | tf_op jit(solution)/shard_map/convert_element_type | solution.py:15
  303.4 1.6 copy-done.2
  304.9 5.4 %fusion.5 = f32[3,1024,512]{2,1,0:T(8,128)} fusion(bf16[4,1024,1024]{2,1,0:T(8,128)(2,1)S(1)} %copy-done.2, bf16[4,512,1024]{2,1,0:T(8,128)(2,1)S(1)} %convert_element_type.21), kind=kOutput, calls=%fused_computation.16 | convolution fusion | flops 3221225472 | bytes 15728640 | tf_op jit(solution)/shard_map/kro,co->krc/dot_general | solution.py:26
  310.3 7.2 %fusion.2 = f32[3,512,1024]{1,2,0:T(8,128)} fusion(bf16[4,512,1024]{2,1,0:T(8,128)(2,1)S(1)} %convert_element_type.21, bf16[4,1024,1024]{2,1,0:T(8,128)(2,1)} %subtract_convert_fusion), kind=kOutput, calls=%fused_computation.9 | convolution fusion | flops 3221225472 | bytes 12582912 | tf_op jit(solution)/shard_map/ro,kco->krc/dot_general | solution.py:32
  317.5 0.0 slice-done
  317.5 0.0 slice-done.1
  317.5 5.5 %fusion.6 = f32[3,1024,512]{2,1,0:T(8,128)} fusion(bf16[4,1024,1024]{2,1,0:T(8,128)(2,1)S(1)} %bitcast.40, bf16[4,512,1024]{2,1,0:T(8,128)(2,1)S(1)} %convert_element_type.21), kind=kOutput, calls=%fused_computation.17 | convolution fusion | flops 3221225472 | bytes 15728640 | tf_op jit(solution)/shard_map/kro,co->krc/dot_general | solution.py:26
  323.0 0.0 copy-done.1
  323.0 5.4 %fusion.3 = f32[3,512,1024]{1,2,0:T(8,128)} fusion(bf16[4,512,1024]{2,1,0:T(8,128)(2,1)S(1)} %convert_element_type.21, bf16[4,1024,1024]{2,1,0:T(8,128)(2,1)S(1)} %bitcast.40), kind=kOutput, calls=%fused_computation.11 | convolution fusion | flops 3221225472 | bytes 12582912 | tf_op jit(solution)/shard_map/ro,kco->krc/dot_general | solution.py:32
  328.4 6.2 %subtract_convert_fusion.1 = bf16[4,512,1024]{2,1,0:T(8,128)(2,1)S(1)} fusion(f32[4,512,1024]{2,1,0:T(8,128)} %all-reduce.2.cloned.1.call-done, bf16[4,512,1024]{2,1,0:T(8,128)(2,1)} %copy-done.1), kind=kLoop, calls=%fused_computation.1 | loop fusion | flops 6291456 | bytes 16777216 | tf_op jit(solution)/shard_map/convert_element_type | solution.py:17
  334.6 5.4 %fusion.4 = f32[3,1024,512]{2,1,0:T(8,128)} fusion(bf16[4,1024,1024]{2,1,0:T(8,128)(2,1)S(1)} %bitcast.40, bf16[4,512,1024]{2,1,0:T(8,128)(2,1)S(1)} %subtract_convert_fusion.1), kind=kOutput, calls=%fused_computation.13 | convolution fusion | flops 3221225472 | bytes 15728640 | tf_op jit(solution)/shard_map/kro,co->krc/dot_general | solution.py:26
  340.0 14.3 %bitcast_add_fusion = f32[3,1024,512]{2,1,0:T(8,128)} fusion(f32[3,1024,512]{2,1,0:T(8,128)} %fusion.5, f32[3,512,1024]{1,2,0:T(8,128)} %fusion.2, f32[3,1024,512]{2,1,0:T(8,128)} %fusion.4, f32[3,1024,512]{2,1,0:T(8,128)} %fusion.6, f32[3,512,1024]{1,2,0:T(8,128)} %fusion.3, bf16[4,512,1024]{2,1,0:T(8,128)(2,1)S(1)} %subtract_convert_fusion.1, ...), kind=kOutput, calls=%fused_computation.3 | convolution fusion | flops 3229089792 | bytes 44040192 | tf_op jit(solution)/shard_map/ro,kco->krc/dot_general | solution.py:32
  (5 shorter events, 0.0 us)
Async XLA Ops:
  6.5 97.6 %all-gather.2.cloned.1.call-start = ((), (), s32[]{:S(2)}) async-start(), calls=%async_computation | async-start | bytes 17825792 | tf_op jit(solution)/shard_map/all_gather | solution.py:46
  8.9 290.3 %all-reduce.2.cloned.1.call-start = ((), (), s32[]{:S(2)}) async-start(), calls=%async_computation.1 | async-start | bytes 16777216 | tf_op jit(solution)/shard_map/psum | solution.py:11
  119.3 3.5 copy-start
  299.1 5.8 %copy-start.2 = (bf16[4,1024,1024]{2,1,0:T(8,128)(2,1)S(1)}, bf16[4,1024,1024]{2,1,0:T(8,128)(2,1)}, u32[]{:S(2)}) copy-start(bf16[4,1024,1024]{2,1,0:T(8,128)(2,1)} %subtract_convert_fusion) | copy-start | bytes 25165828
  304.9 18.1 %copy-start.1 = (bf16[4,512,1024]{2,1,0:T(8,128)(2,1)}, bf16[4,512,1024]{2,1,0:T(8,128)(2,1)S(1)}, u32[]{:S(2)}) copy-start(bf16[4,512,1024]{2,1,0:T(8,128)(2,1)S(1)} %convert_element_type.21) | copy-start | bytes 12582916
  304.9 12.6 %slice-start = ((s8[8388608]{0:T(1024)(128)(4,1)}), s8[4194304]{0:T(1024)(128)(4,1)S(1)}, s32[]{:S(2)}) async-start(s8[8388608]{0:T(1024)(128)(4,1)} %bitcast.39), calls=%async_computation.2 | async-start | bytes 8388608
  310.3 7.2 %slice-start.1 = ((s8[8388608]{0:T(1024)(128)(4,1)}), s8[4194304]{0:T(1024)(128)(4,1)S(1)}, s32[]{:S(2)}) async-start(s8[8388608]{0:T(1024)(128)(4,1)} %bitcast.39), calls=%async_computation.3 | async-start | bytes 8388608
Sparse Core Ops, SparseCore 0:
  9.0 95.1 all-gather.1
  112.8 186.2 all-reduce.1
where the time goes:
time: 361 us
  waiting for transfers between devices  261 us (72%)
  matrix products  43.2 us (12%)
  other arithmetic  38 us (11%)
  between operations  13.5 us (4%)
  local copies, waits for them, and re-layouts  5.1 us (1%)
    psum x1, waiting for transfers between devices, broadcast(): return lax.psum(kept, axis)  166 us
    all_gather x1, waiting for transfers between devices, shards(): row_panel = lax.all_gather(stacked, 'col', axis=1, tiled=True)  95.2 us
    dot_general x3, matrix products, contribute(): jnp.einsum('ro,kco->krc', row_slices[right_index][perturbations], column_...  27 us
    convert_element_type x2, other arithmetic, split_slices(): trailing = lax.optimization_barrier(remainder.astype(jnp.bfloat16))  16.4 us
    dot_general x3, matrix products, contribute(): jnp.einsum('kro,co->krc', row_slices[left_index][:perturbations], column_...  16.3 us
    convert_element_type x2, other arithmetic, split_slices(): leading = lax.optimization_barrier(values.astype(jnp.bfloat16))  10.8 us
    select_n x1, other arithmetic, broadcast(): jnp.where(lax.axis_index(axis) == source, value, 0).astype(value.dtype)  8.5 us
  transfers between devices with their start and end apart: 2, of which 2 were waited for; matrix products, arithmetic and copies ran while one was open for 5% of the time, Pallas kernels for 0%

commit v1 on v0

v1 whole, which is shorter than its diff:
```python
import functools

import jax
import jax.numpy as jnp
from jax import lax
from jax.experimental import pallas as pl
from jax.experimental.pallas import tpu as pltpu
from jax.sharding import PartitionSpec as P

MESH = pl.DeviceIdType.MESH
CHUNKS = 8
ROW_SHARDS = 16
COLUMN_SHARDS = 8
SHARDS = ROW_SHARDS + COLUMN_SHARDS

FROM_LEFT, FROM_RIGHT, FROM_PAIR = 0, 1, 2
LEFT_FAR, RIGHT_FAR = 3, 4
PAIR_LEFT, PAIR_RIGHT = 5, 6
PAIR_LEFT_FAR, PAIR_RIGHT_FAR = 7, 8
PLANE_EVENTS = 9
ROW_BASE = 0
COLUMN_BASE = PLANE_EVENTS
CORE_BASE = 2 * PLANE_EVENTS
CORE_OWN = CORE_BASE + PLANE_EVENTS
TURNED = CORE_OWN + 1
EVENTS = TURNED + 1


def kernel(response_ref, occupied_ref, density_ref, land, high, low, total, load_sem, send_sem, recv_sem, out_sem):
    perturbations, rows, occupied = response_ref.shape
    chunks, _, arrays, _, depth = land.shape
    row, col = lax.axis_index("row"), lax.axis_index("col")
    h, z = row // 4, row % 4
    x, l, c = col // 4, (col // 2) % 2, col % 2

    def device(h_, z_, x_, l_, c_):
        return (h_ * 4 + z_, x_ * 4 + l_ * 2 + c_)

    right, left = device(h, z, (x + 1) % 4, l, c), device(h, z, (x + 3) % 4, l, c)
    near = device(h, z, x, 1 - l, c)
    up, down = device(h, (z + 1) % 4, x, l, c), device(h, (z + 3) % 4, x, l, c)
    across = device(1 - h, z, x, l, c)
    twin = device(h, z, x, l, 1 - c)
    turned_h = (h + x + jnp.where(row == 0, 1, 0)) % 2
    turn_to = (turned_h * 4 + (z + col % 4) % 4, row * 2 + col // 8)
    group = col // 2
    source_h, source_z = group // 4, group % 4
    odd = jnp.where(group == 0, 1, 0)
    source_x = 2 * c + (h + source_h + odd) % 2
    turn_from = (group, source_x * 4 + (z + 4 - source_z) % 4)

    def row_slot(step, flip):
        return ((x + step) % 4) * 4 + ((l + flip) % 2) * 2 + c

    def column_slot(step, flip):
        return ROW_SHARDS + ((h + flip + source_h + odd) % 2) * 4 + (z + step + 4 - source_z) % 4

    barrier = pltpu.get_barrier_semaphore()
    peers = (right, left, near, up, down, across, twin, turn_to, turn_from)
    for peer in peers:
        pl.semaphore_signal(barrier, inc=1, device_id=peer, device_id_type=MESH)

    def load(chunk):
        columns = pl.ds(pl.multiple_of(chunk * depth, depth), depth)
        return (
            pltpu.make_async_copy(response_ref.at[:, :, columns], land.at[chunk, col, pl.ds(0, perturbations)], load_sem.at[chunk, 0]),
            pltpu.make_async_copy(occupied_ref.at[:, columns], land.at[chunk, col, perturbations], load_sem.at[chunk, 1]),
        )

    @pl.loop(0, chunks)
    def _(chunk):
        for copy in load(chunk):
            copy.start()

    def part(chunk, slot, half):
        if half is None:
            return land.at[chunk, slot]
        return land.at[chunk, slot, pl.ds(half * (arrays // 2), arrays // 2)]

    def transfer(chunk, source, slot, event, peer, half=None):
        return pltpu.make_async_remote_copy(
            src_ref=part(chunk, source, half),
            dst_ref=part(chunk, slot, half),
            send_sem=send_sem.at[chunk],
            recv_sem=recv_sem.at[chunk, event],
            device_id=peer,
            device_id_type=MESH,
        )

    def send(chunk, slot, event, peer, half=None):
        transfer(chunk, slot, slot, event, peer, half).start()

    def arrived(chunk, slot, event, half=None):
        transfer(chunk, slot, slot, event, twin, half).wait_recv()

    def begin(chunk):
        for copy in load(chunk):
            copy.wait()
        transfer(chunk, col, ROW_SHARDS + col % 8, TURNED, turn_to).start()
        send(chunk, col, ROW_BASE + FROM_LEFT, right)
        send(chunk, col, ROW_BASE + FROM_RIGHT, left)
        send(chunk, col, ROW_BASE + FROM_PAIR, near)
        send(chunk, col, CORE_OWN, twin)

    def turn(chunk):
        slot = column_slot(0, 0)
        arrived(chunk, slot, TURNED)
        send(chunk, slot, COLUMN_BASE + FROM_LEFT, up)
        send(chunk, slot, COLUMN_BASE + FROM_RIGHT, down)
        send(chunk, slot, COLUMN_BASE + FROM_PAIR, across)

    def relay(chunk, slot, base, event, forward, half=None):
        arrived(chunk, slot, base + event, half)
        for next_event, peer, next_half in forward:
            send(chunk, slot, base + next_event, peer, next_half)
        if base == ROW_BASE:
            send(chunk, slot, CORE_BASE + event, twin, half)

    def first(chunk):
        for base, slot, ahead, behind in ((ROW_BASE, row_slot, right, left), (COLUMN_BASE, column_slot, up, down)):
            relay(chunk, slot(3, 0), base, FROM_LEFT, ((LEFT_FAR, ahead, 0),))
            relay(chunk, slot(1, 0), base, FROM_RIGHT, ((RIGHT_FAR, behind, 1),))
            relay(chunk, slot(0, 1), base, FROM_PAIR, ((PAIR_LEFT, ahead, None), (PAIR_RIGHT, behind, None)))

    def second(chunk):
        for base, slot, ahead, behind in ((ROW_BASE, row_slot, right, left), (COLUMN_BASE, column_slot, up, down)):
            relay(chunk, slot(2, 0), base, LEFT_FAR, (), 0)
            relay(chunk, slot(2, 0), base, RIGHT_FAR, (), 1)
            relay(chunk, slot(3, 1), base, PAIR_LEFT, ((PAIR_LEFT_FAR, ahead, 0),))
            relay(chunk, slot(1, 1), base, PAIR_RIGHT, ((PAIR_RIGHT_FAR, behind, 1),))

    def third(chunk):
        for base, slot in ((ROW_BASE, row_slot), (COLUMN_BASE, column_slot)):
            relay(chunk, slot(2, 1), base, PAIR_LEFT_FAR, (), 0)
            relay(chunk, slot(2, 1), base, PAIR_RIGHT_FAR, (), 1)

    def other(step, flip):
        return ((x + step) % 4) * 4 + ((l + flip) % 2) * 2 + 1 - c

    def fourth(chunk):
        arrived(chunk, other(0, 0), CORE_OWN)
        arrived(chunk, other(3, 0), CORE_BASE + FROM_LEFT)
        arrived(chunk, other(1, 0), CORE_BASE + FROM_RIGHT)
        arrived(chunk, other(0, 1), CORE_BASE + FROM_PAIR)
        arrived(chunk, other(2, 0), CORE_BASE + LEFT_FAR, 0)
        arrived(chunk, other(2, 0), CORE_BASE + RIGHT_FAR, 1)
        arrived(chunk, other(3, 1), CORE_BASE + PAIR_LEFT)
        arrived(chunk, other(1, 1), CORE_BASE + PAIR_RIGHT)
        arrived(chunk, other(2, 1), CORE_BASE + PAIR_LEFT_FAR, 0)
        arrived(chunk, other(2, 1), CORE_BASE + PAIR_RIGHT_FAR, 1)

    def split(chunk):
        @pl.loop(0, SHARDS)
        def _(shard):
            values = land[chunk, shard]
            leading = values.astype(jnp.bfloat16)
            trailing = (values - leading.astype(jnp.float32)).astype(jnp.bfloat16)
            where = pl.ds(pl.multiple_of(shard * rows, rows), rows)
            high[:, where, :] = leading
            low[:, where, :] = trailing

    columns_out = COLUMN_SHARDS * rows
    rows_out = ROW_SHARDS * rows
    tile = 256

    def multiply(k):
        there = pl.ds(rows_out, columns_out)
        right_side = jnp.concatenate(
            [high[perturbations, there], low[perturbations, there], high[perturbations, there], high[k, there], high[k, there], low[k, there]], axis=1
        )

        @pl.loop(0, rows_out // tile)
        def _(m):
            here = pl.ds(pl.multiple_of(m * tile, tile), tile)
            left_side = jnp.concatenate(
                [high[k, here], high[k, here], low[k, here], high[perturbations, here], low[perturbations, here], high[perturbations, here]], axis=1
            )
            total[k, here, :] += lax.dot_general(
                left_side, right_side, (((1,), (1,)), ((), ())), preferred_element_type=jnp.float32
            )

    pl.semaphore_wait(barrier, len(peers))
    begin(0)
    begin(1)

    @pl.loop(0, perturbations)
    def _(k):
        total[k] = jnp.zeros(total.shape[1:], jnp.float32)

    turn(0)
    first(0)

    @pl.loop(0, chunks)
    def _(chunk):
        @pl.when(chunk + 2 < chunks)
        def _():
            begin(chunk + 2)

        @pl.when(chunk + 1 < chunks)
        def _():
            turn(chunk + 1)

        second(chunk)

        @pl.when(chunk + 1 < chunks)
        def _():
            first(chunk + 1)

        third(chunk)
        fourth(chunk)
        split(chunk)

        @pl.loop(0, perturbations)
        def _(k):
            multiply(k)

            @pl.when(chunk == chunks - 1)
            def _():
                pltpu.make_async_copy(total.at[k], density_ref.at[k], out_sem.at[k]).start()

    @pl.loop(0, chunks)
    def _(chunk):
        sent = land.at[chunk, pl.ds(0, SHARDS - 1)]
        pltpu.make_async_copy(sent, sent, send_sem.at[chunk]).wait()

    for k in range(perturbations):
        pltpu.make_async_copy(total.at[k], density_ref.at[k], out_sem.at[k]).wait()


def shards(response_coeffs, occupied_coeffs):
    perturbations, rows, occupied = response_coeffs.shape
    depth = occupied // CHUNKS
    return pl.pallas_call(
        kernel,
        name="gather_multiply",
        out_shape=jax.ShapeDtypeStruct((perturbations, ROW_SHARDS * rows, COLUMN_SHARDS * rows), jnp.float32),
        in_specs=[pl.BlockSpec(memory_space=pl.ANY)] * 2,
        out_specs=pl.BlockSpec(memory_space=pl.ANY),
        scratch_shapes=[
            pltpu.VMEM((CHUNKS, SHARDS, perturbations + 1, rows, depth), jnp.float32),
            pltpu.VMEM((perturbations + 1, SHARDS * rows, depth), jnp.bfloat16),
            pltpu.VMEM((perturbations + 1, SHARDS * rows, depth), jnp.bfloat16),
            pltpu.VMEM((perturbations, ROW_SHARDS * rows, COLUMN_SHARDS * rows), jnp.float32),
            pltpu.SemaphoreType.DMA((CHUNKS, 2)),
            pltpu.SemaphoreType.DMA((CHUNKS,)),
            pltpu.SemaphoreType.DMA((CHUNKS, EVENTS)),
            pltpu.SemaphoreType.DMA((perturbations,)),
        ],
        compiler_params=pltpu.CompilerParams(
            collective_id=0, has_side_effects=True, vmem_limit_bytes=56 * 1024 * 1024
        ),
    )(response_coeffs, occupied_coeffs)


def solution(mesh):
    return jax.shard_map(
        shards,
        mesh=mesh,
        in_specs=(P(None, ("row", "col"), None), P(("row", "col"), None)),
        out_specs=P(None, "row", "col"),
        check_vma=False,
    )
```

time: 361 us -> 185 us (0.51)
  waiting for transfers between devices: 261 us -> 0 us
  Pallas kernels: 0 us -> 179 us
  matrix products: 43.2 us -> 0 us
  other arithmetic: 38 us -> 0 us
  between operations: 13.5 us -> 0.01 us
    pallas_call x0 -> x1, Pallas kernels: none -> 179 us  [shards(): pl.pallas_call(kernel, name='gather_multiply', out_shape=jax.ShapeDtypeSt...]
    psum x1 -> x0, waiting for transfers between devices: 166 us -> none  [broadcast(): return lax.psum(kept, axis)]
    all_gather x1 -> x0, waiting for transfers between devices: 95.2 us -> none  [shards(): row_panel = lax.all_gather(stacked, 'col', axis=1, tiled=True)]
    dot_general x6 -> x0, matrix products: 43.2 us -> none  [the longest x3 27 us: contribute(): jnp.einsum('ro,kco->krc', row_slices[right_index][perturbations], column_...]
    convert_element_type x4 -> x0, other arithmetic: 27.2 us -> none  [the longest x2 16.4 us: split_slices(): trailing = lax.optimization_barrier(remainder.astype(jnp.bfloat16))]
    select_n x1 -> x0, other arithmetic: 8.5 us -> none  [broadcast(): jnp.where(lax.axis_index(axis) == source, value, 0).astype(value.dtype)]
  transfers between devices with their start and end apart: 2 -> 0, of which waited for: 2 -> 0; matrix products, arithmetic and copies ran while one was open for 5% -> 0% of each run, Pallas kernels for 0% -> 0%
where the time goes in v1:
time: 185 us
  Pallas kernels  179 us (97%)
  local copies, waits for them, and re-layouts  6.2 us (3%)
    pallas_call x1, Pallas kernels, shards(): pl.pallas_call(kernel, name='gather_multiply', out_shape=jax.ShapeDtypeSt...  179 us
    unnamed x1, local copies, waits for them, and re-layouts  6.2 us

profile of v1, /device:TPU:1, one launch (start us, length us, event | category | flops | bytes accessed | tf_op | source)
XLA Modules:
  0.0 185.3 jit_solution(14579581305680123140)
XLA Ops:
  0.0 179.1 %gather_multiply.1 = f32[3,1024,512]{2,1,0:T(8,128)} custom-call(f32[3,64,1024]{2,1,0:T(8,128)} %response_ref.1, f32[64,1024]{1,0:T(8,128)} %occupied_ref.1), custom_call_target="tpu_custom_call" | custom-call | tf_op jit(solution)/shard_map/gather_multiply/pallas_call | solution.py:233
  179.1 6.2 %copy.4 = f32[3,1024,512]{2,1,0:T(8,128)} copy(f32[3,1024,512]{2,1,0:T(8,128)} %gather_multiply.1) | data formatting | bytes 12582912

commit v2 on v1

v2 whole, which is shorter than its diff:
```python
import functools

import jax
import jax.numpy as jnp
from jax import lax
from jax.experimental import pallas as pl
from jax.experimental.pallas import tpu as pltpu
from jax.sharding import PartitionSpec as P

MESH = pl.DeviceIdType.MESH
CHUNKS = 8
ROW_SHARDS = 16
COLUMN_SHARDS = 8
SHARDS = ROW_SHARDS + COLUMN_SHARDS
TURN_SLOTS = 2

LEFT, RIGHT, PAIR, LEFT_FAR, RIGHT_FAR = 0, 1, 2, 3, 4
PAIR_LEFT, PAIR_RIGHT, PAIR_LEFT_FAR, PAIR_RIGHT_FAR = 5, 6, 7, 8
PLANE_EVENTS = 9
ROW_BASE = 0
COLUMN_BASE = PLANE_EVENTS
CORE_BASE = 2 * PLANE_EVENTS
CORE_OWN = 3 * PLANE_EVENTS
TURN_BASE = CORE_OWN + 1
EVENTS = TURN_BASE + 3


def kernel(response_ref, occupied_ref, density_ref, land, high, low, total, load_sem, send_sem, turn_sem, recv_sem, out_sem):
    perturbations, rows, occupied = response_ref.shape
    chunks, _, arrays, _, depth = land.shape
    row, col = lax.axis_index("row"), lax.axis_index("col")
    h, z = row // 4, row % 4
    x, l, c = col // 4, (col // 2) % 2, col % 2

    def device(h_, z_, x_, l_, c_):
        return (h_ * 4 + z_ % 4, (x_ % 4) * 4 + l_ * 2 + c_)

    def along_x(step):
        return device(h, z, x + step, l, c)

    def along_z(step):
        return device(h, z + step, x, l, c)

    near = device(h, z, x, 1 - l, c)
    across = device(1 - h, z, x, l, c)
    twin = device(h, z, x, l, 1 - c)

    def differs(a, b):
        return jnp.logical_or(a[0] != b[0], a[1] != b[1])

    here = device(h, z, x, l, c)
    offset = 2 * c + l
    moved_z = offset != 0
    z_mid = (z + 4 - offset) % 4
    to_y = device((h + x) % 2, z, x, z_mid % 2, c)
    l_y = (z + l) % 2
    z_y = (z + 8 - 2 * c - l_y) % 4
    h_y = (h + x) % 2
    from_y = device(h_y, z, x, l_y, c)
    to_x = device(h, z, h_y * 2 + z_y // 2, l, x // 2)
    h_s, z_s = x // 2, (x % 2) * 2 + l
    offset_s = (z + 4 - z_s) % 4
    x_s = c * 2 + (h + h_s) % 2
    from_x = device(h, z, x_s, l, offset_s // 2)
    goes_y, came_y = differs(here, to_y), differs(here, from_y)
    goes_x, came_x = differs(here, to_x), differs(here, from_x)

    def column_slot(step, flip):
        there = (z + step + 4 - z_s) % 4
        return ROW_SHARDS + ((h + flip + h_s) % 2) * 4 + (there % 2) * 2 + there // 2

    def row_slot(step, flip, core):
        return ((x + step) % 4) * 4 + ((l + flip) % 2) * 2 + core

    place_z = jnp.where(moved_z, SHARDS, col)
    place_y = jnp.where(came_y, SHARDS + 1, place_z)
    own_column = column_slot(0, 0)
    place_x = jnp.where(came_x, own_column, place_y)

    barrier = pltpu.get_barrier_semaphore()
    peers = [along_x(1), along_x(3), along_z(1), along_z(3), along_z(2)] + [near, across, twin]
    peers += [device(1 - h, z, x, 1 - l, c)] + [device(h, z, x + s, l, 1 - c) for s in (1, 2, 3)] + [along_x(2)]
    for peer in peers:
        pl.semaphore_signal(barrier, inc=1, device_id=peer, device_id_type=MESH)

    def load(chunk):
        columns = pl.ds(pl.multiple_of(chunk * depth, depth), depth)
        return (
            pltpu.make_async_copy(response_ref.at[:, :, columns], land.at[chunk, col, pl.ds(0, perturbations)], load_sem.at[chunk, 0]),
            pltpu.make_async_copy(occupied_ref.at[:, columns], land.at[chunk, col, perturbations], load_sem.at[chunk, 1]),
        )

    @pl.loop(0, chunks)
    def _(chunk):
        for copy in load(chunk):
            copy.start()

    def part(chunk, slot, half):
        if half is None:
            return land.at[chunk, slot]
        return land.at[chunk, slot, pl.ds(half * (arrays // 2), arrays // 2)]

    def transfer(chunk, source, slot, event, peer, sem=None, half=None):
        return pltpu.make_async_remote_copy(
            src_ref=part(chunk, source, half),
            dst_ref=part(chunk, slot, half),
            send_sem=send_sem.at[chunk] if sem is None else sem,
            recv_sem=recv_sem.at[chunk, event],
            device_id=peer,
            device_id_type=MESH,
        )

    def send(chunk, source, slot, event, peer, half=None):
        transfer(chunk, source, slot, event, peer, None, half).start()

    def arrived(chunk, slot, event, half=None):
        transfer(chunk, slot, slot, event, twin, None, half).wait_recv()

    def turn_z(chunk):
        return transfer(chunk, col, SHARDS, TURN_BASE, along_z(offset), turn_sem.at[chunk, 0])

    def turn_y(chunk):
        return transfer(chunk, place_z, SHARDS + 1, TURN_BASE + 1, to_y, turn_sem.at[chunk, 1])

    def turn_x(chunk):
        x_to, c_to = h_y * 2 + z_y // 2, x // 2
        slot = ROW_SHARDS + (x % 2) * 4 + l_y * 2 + c
        return transfer(chunk, place_y, slot, TURN_BASE + 2, to_x, turn_sem.at[chunk, 2])

    def begin(chunk):
        send(chunk, col, col, ROW_BASE + PAIR, near)
        send(chunk, col, col, ROW_BASE + LEFT, along_x(1))
        send(chunk, col, col, ROW_BASE + RIGHT, along_x(3))
        send(chunk, col, col, CORE_OWN, twin)

    def turn_first(chunk):
        for copy in load(chunk):
            copy.wait()

        @pl.when(moved_z)
        def _():
            turn_z(chunk).start()

    def turn_second(chunk):
        @pl.when(moved_z)
        def _():
            turn_z(chunk).wait_recv()

        @pl.when(goes_y)
        def _():
            turn_y(chunk).start()

    def turn_third(chunk):
        @pl.when(came_y)
        def _():
            turn_y(chunk).wait_recv()

        @pl.when(goes_x)
        def _():
            turn_x(chunk).start()

    def turned(chunk):
        @pl.when(came_x)
        def _():
            arrived(chunk, own_column, TURN_BASE + 2)

        send(chunk, place_x, own_column, COLUMN_BASE + PAIR, across)
        send(chunk, place_x, own_column, COLUMN_BASE + LEFT, along_z(1))
        send(chunk, place_x, own_column, COLUMN_BASE + RIGHT, along_z(3))

    def relay(chunk, slot, base, event, forward, half=None):
        arrived(chunk, slot, base + event, half)
        for next_event, peer, next_half in forward:
            send(chunk, slot, slot, base + next_event, peer, next_half)
        if base == ROW_BASE:
            send(chunk, slot, slot, CORE_BASE + event, twin, half)

    def row_place(step, flip):
        return row_slot(step, flip, c)

    planes = ((ROW_BASE, row_place, along_x), (COLUMN_BASE, column_slot, along_z))

    def first(plane, chunk):
        base, slot, along = plane
        relay(chunk, slot(0, 1), base, PAIR, ((PAIR_LEFT, along(1), None), (PAIR_RIGHT, along(3), None)))
        relay(chunk, slot(3, 0), base, LEFT, ((LEFT_FAR, along(1), 0),))
        relay(chunk, slot(1, 0), base, RIGHT, ((RIGHT_FAR, along(3), 1),))

    def second(plane, chunk):
        base, slot, along = plane
        relay(chunk, slot(3, 1), base, PAIR_LEFT, ((PAIR_LEFT_FAR, along(1), 0),))
        relay(chunk, slot(1, 1), base, PAIR_RIGHT, ((PAIR_RIGHT_FAR, along(3), 1),))
        relay(chunk, slot(2, 0), base, LEFT_FAR, (), 0)
        relay(chunk, slot(2, 0), base, RIGHT_FAR, (), 1)

    def third(plane, chunk):
        base, slot, along = plane
        relay(chunk, slot(2, 1), base, PAIR_LEFT_FAR, (), 0)
        relay(chunk, slot(2, 1), base, PAIR_RIGHT_FAR, (), 1)

    row_first, column_first = functools.partial(first, planes[0]), functools.partial(first, planes[1])
    row_second, column_second = functools.partial(second, planes[0]), functools.partial(second, planes[1])
    row_third, column_third = functools.partial(third, planes[0]), functools.partial(third, planes[1])

    def from_twin(chunk):
        arrived(chunk, row_slot(0, 0, 1 - c), CORE_OWN)
        for step, flip, event, half in (
            (0, 1, PAIR, None), (3, 0, LEFT, None), (1, 0, RIGHT, None), (3, 1, PAIR_LEFT, None), (1, 1, PAIR_RIGHT, None),
            (2, 0, LEFT_FAR, 0), (2, 0, RIGHT_FAR, 1), (2, 1, PAIR_LEFT_FAR, 0), (2, 1, PAIR_RIGHT_FAR, 1),
        ):
            arrived(chunk, row_slot(step, flip, 1 - c), CORE_BASE + event, half)

    def split(chunk):
        @pl.loop(0, SHARDS)
        def _(shard):
            values = land[chunk, jnp.where(shard == own_column, place_x, shard)]
            leading = values.astype(jnp.bfloat16)
            trailing = (values - leading.astype(jnp.float32)).astype(jnp.bfloat16)
            where = pl.ds(pl.multiple_of(shard * rows, rows), rows)
            high[:, where, :] = leading
            low[:, where, :] = trailing

    rows_out = ROW_SHARDS * rows

    def multiply(k):
        ours, theirs = slice(0, rows_out), slice(rows_out, SHARDS * rows)
        o = perturbations
        left_side = jnp.concatenate(
            [high[k, ours], high[k, ours], low[k, ours], high[o, ours], low[o, ours], high[o, ours]], axis=1
        )
        right_side = jnp.concatenate(
            [high[o, theirs], low[o, theirs], high[o, theirs], high[k, theirs], high[k, theirs], low[k, theirs]], axis=1
        )
        total[k] += lax.dot_general(
            left_side, right_side, (((1,), (1,)), ((), ())), preferred_element_type=jnp.float32
        )

    def ahead(chunk, step):
        pl.when(chunk < chunks)(lambda: step(chunk))

    pl.semaphore_wait(barrier, len(peers))
    for chunk in range(3):
        turn_first(chunk)
    begin(0)

    @pl.loop(3, chunks)
    def _(chunk):
        turn_first(chunk)

    turn_second(0)
    turn_second(1)
    begin(1)
    turn_second(2)
    turn_third(0)
    row_first(0)
    turn_second(3)
    turn_third(1)
    turned(0)
    begin(2)

    @pl.loop(0, perturbations)
    def _(k):
        total[k] = jnp.zeros(total.shape[1:], jnp.float32)

    row_second(0)
    row_first(1)
    turn_second(4)
    turn_third(2)
    turned(1)
    column_first(0)
    turn_second(5)
    turn_third(3)
    turned(2)
    column_second(0)
    column_first(1)

    @pl.loop(0, chunks)
    def _(chunk):
        ahead(chunk + 1, row_second)
        ahead(chunk + 2, row_first)
        ahead(chunk + 3, begin)
        ahead(chunk + 6, turn_second)
        ahead(chunk + 4, turn_third)
        ahead(chunk + 3, turned)
        ahead(chunk + 1, column_second)
        ahead(chunk + 2, column_first)
        row_third(chunk)
        column_third(chunk)
        from_twin(chunk)
        split(chunk)

        @pl.loop(0, perturbations)
        def _(k):
            multiply(k)

            @pl.when(chunk == chunks - 1)
            def _():
                pltpu.make_async_copy(total.at[k], density_ref.at[k], out_sem.at[k]).start()

    @pl.loop(0, chunks)
    def _(chunk):
        sent = land.at[chunk, pl.ds(0, 22)]
        pltpu.make_async_copy(sent, sent, send_sem.at[chunk]).wait()
        pl.when(moved_z)(lambda: turn_z(chunk).wait_send())
        pl.when(goes_y)(lambda: turn_y(chunk).wait_send())
        pl.when(goes_x)(lambda: turn_x(chunk).wait_send())

    for k in range(perturbations):
        pltpu.make_async_copy(total.at[k], density_ref.at[k], out_sem.at[k]).wait()


def shards(response_coeffs, occupied_coeffs):
    perturbations, rows, occupied = response_coeffs.shape
    depth = occupied // CHUNKS
    return pl.pallas_call(
        kernel,
        name="gather_multiply",
        out_shape=jax.ShapeDtypeStruct((perturbations, ROW_SHARDS * rows, COLUMN_SHARDS * rows), jnp.float32),
        in_specs=[pl.BlockSpec(memory_space=pl.ANY)] * 2,
        out_specs=pl.BlockSpec(memory_space=pl.ANY),
        scratch_shapes=[
            pltpu.VMEM((CHUNKS, SHARDS + TURN_SLOTS, perturbations + 1, rows, depth), jnp.float32),
            pltpu.VMEM((perturbations + 1, SHARDS * rows, depth), jnp.bfloat16),
            pltpu.VMEM((perturbations + 1, SHARDS * rows, depth), jnp.bfloat16),
            pltpu.VMEM((perturbations, ROW_SHARDS * rows, COLUMN_SHARDS * rows), jnp.float32),
            pltpu.SemaphoreType.DMA((CHUNKS, 2)),
            pltpu.SemaphoreType.DMA((CHUNKS,)),
            pltpu.SemaphoreType.DMA((CHUNKS, 3)),
            pltpu.SemaphoreType.DMA((CHUNKS, EVENTS)),
            pltpu.SemaphoreType.DMA((perturbations,)),
        ],
        compiler_params=pltpu.CompilerParams(
            collective_id=0, has_side_effects=True, vmem_limit_bytes=56 * 1024 * 1024
        ),
    )(response_coeffs, occupied_coeffs)


def solution(mesh):
    return jax.shard_map(
        shards,
        mesh=mesh,
        in_specs=(P(None, ("row", "col"), None), P(("row", "col"), None)),
        out_specs=P(None, "row", "col"),
        check_vma=False,
    )
```

time: 185 us -> 119 us (0.64)
  Pallas kernels: 179 us -> 112 us
    pallas_call x1, Pallas kernels: 179 us -> 112 us  [shards(): pl.pallas_call(kernel, name='gather_multiply', out_shape=jax.ShapeDtypeSt...]
where the time goes in v2:
time: 119 us; the launch traced here: 118 us
  Pallas kernels  112 us (94%)
  local copies, waits for them, and re-layouts  6.2 us (5%)
    pallas_call x1, Pallas kernels, shards(): pl.pallas_call(kernel, name='gather_multiply', out_shape=jax.ShapeDtypeSt...  112 us
    unnamed x1, local copies, waits for them, and re-layouts  6.2 us

profile of v2, /device:TPU:1, one launch (start us, length us, event | category | flops | bytes accessed | tf_op | source)
XLA Modules:
  0.0 118.4 jit_solution(8684044809100242755)
XLA Ops:
  0.0 112.2 %gather_multiply.1 = f32[3,1024,512]{2,1,0:T(8,128)} custom-call(f32[3,64,1024]{2,1,0:T(8,128)} %response_ref.1, f32[64,1024]{1,0:T(8,128)} %occupied_ref.1), custom_call_target="tpu_custom_call" | custom-call | tf_op jit(solution)/shard_map/gather_multiply/pallas_call | solution.py:315
  112.2 6.2 %copy.4 = f32[3,1024,512]{2,1,0:T(8,128)} copy(f32[3,1024,512]{2,1,0:T(8,128)} %gather_multiply.1) | data formatting | bytes 12582912

commit v3 on v2

--- a/solution.py
+++ b/solution.py
@@ -25,7 +25,7 @@
 EVENTS = TURN_BASE + 3
 
 
-def kernel(response_ref, occupied_ref, density_ref, land, high, low, total, load_sem, send_sem, turn_sem, recv_sem, out_sem):
+def kernel(response_ref, occupied_ref, high, low, total, land, load_sem, send_sem, turn_sem, recv_sem):
     perturbations, rows, occupied = response_ref.shape
     chunks, _, arrays, _, depth = land.shape
     row, col = lax.axis_index("row"), lax.axis_index("col")
@@ -49,33 +49,33 @@
         return jnp.logical_or(a[0] != b[0], a[1] != b[1])
 
     here = device(h, z, x, l, c)
-    offset = 2 * c + l
-    moved_z = offset != 0
-    z_mid = (z + 4 - offset) % 4
-    to_y = device((h + x) % 2, z, x, z_mid % 2, c)
-    l_y = (z + l) % 2
-    z_y = (z + 8 - 2 * c - l_y) % 4
-    h_y = (h + x) % 2
-    from_y = device(h_y, z, x, l_y, c)
-    to_x = device(h, z, h_y * 2 + z_y // 2, l, x // 2)
     h_s, z_s = x // 2, (x % 2) * 2 + l
-    offset_s = (z + 4 - z_s) % 4
-    x_s = c * 2 + (h + h_s) % 2
-    from_x = device(h, z, x_s, l, offset_s // 2)
-    goes_y, came_y = differs(here, to_y), differs(here, from_y)
-    goes_x, came_x = differs(here, to_x), differs(here, from_x)
-
-    def column_slot(step, flip):
-        there = (z + step + 4 - z_s) % 4
-        return ROW_SHARDS + ((h + flip + h_s) % 2) * 4 + (there % 2) * 2 + there // 2
+
+    def route(chunk):
+        odd = chunk % 2
+        offset = (2 * c + l + 2 * odd) % 4
+        to_y = device((h + x + odd) % 2, z, x, (z + offset) % 2, c)
+        l_y = (z + l) % 2
+        z_y = (z + 8 - 2 * c - l_y - 2 * odd) % 4
+        h_y = (h + x + odd) % 2
+        from_y = device(h_y, z, x, l_y, c)
+        to_x = device(h, z, h_y * 2 + z_y // 2, l, x // 2)
+        from_x = device(h, z, c * 2 + (h + h_s + odd) % 2, l, (z + 8 - z_s - 2 * odd) % 4 // 2)
+        moved_z, came_y, came_x = offset != 0, differs(here, from_y), differs(here, from_x)
+        goes_y, goes_x = differs(here, to_y), differs(here, to_x)
+        place_z = jnp.where(moved_z, SHARDS, col)
+        place_y = jnp.where(came_y, SHARDS + 1, place_z)
+        place_x = jnp.where(came_x, column_slot(chunk, 0, 0), place_y)
+        slot_x = ROW_SHARDS + (x % 2) * 4 + l_y * 2 + c
+        return offset, to_y, to_x, moved_z, goes_y, came_y, goes_x, came_x, place_z, place_y, place_x, slot_x
+
+    def column_slot(chunk, step, flip):
+        odd = chunk % 2
+        there = (z + step + 8 - z_s - 2 * odd) % 4
+        return ROW_SHARDS + ((h + flip + h_s + odd) % 2) * 4 + (there % 2) * 2 + there // 2
 
     def row_slot(step, flip, core):
         return ((x + step) % 4) * 4 + ((l + flip) % 2) * 2 + core
-
-    place_z = jnp.where(moved_z, SHARDS, col)
-    place_y = jnp.where(came_y, SHARDS + 1, place_z)
-    own_column = column_slot(0, 0)
-    place_x = jnp.where(came_x, own_column, place_y)
 
     barrier = pltpu.get_barrier_semaphore()
     peers = [along_x(1), along_x(3), along_z(1), along_z(3), along_z(2)] + [near, across, twin]
@@ -117,15 +117,16 @@
         transfer(chunk, slot, slot, event, twin, None, half).wait_recv()
 
     def turn_z(chunk):
+        offset = route(chunk)[0]
         return transfer(chunk, col, SHARDS, TURN_BASE, along_z(offset), turn_sem.at[chunk, 0])
 
     def turn_y(chunk):
+        _, to_y, _, _, _, _, _, _, place_z, _, _, _ = route(chunk)
         return transfer(chunk, place_z, SHARDS + 1, TURN_BASE + 1, to_y, turn_sem.at[chunk, 1])
 
     def turn_x(chunk):
-        x_to, c_to = h_y * 2 + z_y // 2, x // 2
-        slot = ROW_SHARDS + (x % 2) * 4 + l_y * 2 + c
-        return transfer(chunk, place_y, slot, TURN_BASE + 2, to_x, turn_sem.at[chunk, 2])
+        _, _, to_x, _, _, _, _, _, _, place_y, _, slot_x = route(chunk)
+        return transfer(chunk, place_y, slot_x, TURN_BASE + 2, to_x, turn_sem.at[chunk, 2])
 
     def begin(chunk):
         send(chunk, col, col, ROW_BASE + PAIR, near)
@@ -136,34 +137,23 @@
     def turn_first(chunk):
         for copy in load(chunk):
             copy.wait()
-
-        @pl.when(moved_z)
-        def _():
-            turn_z(chunk).start()
+        moved_z = route(chunk)[3]
+        pl.when(moved_z)(lambda: turn_z(chunk).start())
 
     def turn_second(chunk):
-        @pl.when(moved_z)
-        def _():
-            turn_z(chunk).wait_recv()
-
-        @pl.when(goes_y)
-        def _():
-            turn_y(chunk).start()
+        _, _, _, moved_z, goes_y, _, _, _, _, _, _, _ = route(chunk)
+        pl.when(moved_z)(lambda: turn_z(chunk).wait_recv())
+        pl.when(goes_y)(lambda: turn_y(chunk).start())
 
     def turn_third(chunk):
-        @pl.when(came_y)
-        def _():
-            turn_y(chunk).wait_recv()
-
-        @pl.when(goes_x)
-        def _():
-            turn_x(chunk).start()
+        _, _, _, _, _, came_y, goes_x, _, _, _, _, _ = route(chunk)
+        pl.when(came_y)(lambda: turn_y(chunk).wait_recv())
+        pl.when(goes_x)(lambda: turn_x(chunk).start())
 
     def turned(chunk):
-        @pl.when(came_x)
-        def _():
-            arrived(chunk, own_column, TURN_BASE + 2)
-
+        _, _, _, _, _, _, _, came_x, _, _, place_x, _ = route(chunk)
+        own_column = column_slot(chunk, 0, 0)
+        pl.when(came_x)(lambda: arrived(chunk, own_column, TURN_BASE + 2))
         send(chunk, place_x, own_column, COLUMN_BASE + PAIR, across)
         send(chunk, place_x, own_column, COLUMN_BASE + LEFT, along_z(1))
         send(chunk, place_x, own_column, COLUMN_BASE + RIGHT, along_z(3))
@@ -175,28 +165,35 @@
         if base == ROW_BASE:
             send(chunk, slot, slot, CORE_BASE + event, twin, half)
 
-    def row_place(step, flip):
+    def row_place(chunk, step, flip):
         return row_slot(step, flip, c)
 
     planes = ((ROW_BASE, row_place, along_x), (COLUMN_BASE, column_slot, along_z))
 
     def first(plane, chunk):
         base, slot, along = plane
-        relay(chunk, slot(0, 1), base, PAIR, ((PAIR_LEFT, along(1), None), (PAIR_RIGHT, along(3), None)))
-        relay(chunk, slot(3, 0), base, LEFT, ((LEFT_FAR, along(1), 0),))
-        relay(chunk, slot(1, 0), base, RIGHT, ((RIGHT_FAR, along(3), 1),))
+        relay(chunk, slot(chunk, 0, 1), base, PAIR, ((PAIR_LEFT, along(1), None), (PAIR_RIGHT, along(3), None)))
+        relay(chunk, slot(chunk, 3, 0), base, LEFT, ((LEFT_FAR, along(1), 0),))
+        relay(chunk, slot(chunk, 1, 0), base, RIGHT, ((RIGHT_FAR, along(3), 1),))
 
     def second(plane, chunk):
         base, slot, along = plane
-        relay(chunk, slot(3, 1), base, PAIR_LEFT, ((PAIR_LEFT_FAR, along(1), 0),))
-        relay(chunk, slot(1, 1), base, PAIR_RIGHT, ((PAIR_RIGHT_FAR, along(3), 1),))
-        relay(chunk, slot(2, 0), base, LEFT_FAR, (), 0)
-        relay(chunk, slot(2, 0), base, RIGHT_FAR, (), 1)
+        if base in (COLUMN_BASE,):
+            over = across if base == COLUMN_BASE else near
+            relay(chunk, slot(chunk, 2, 0), base, LEFT_FAR, ((PAIR_LEFT_FAR, over, 0),), 0)
+            relay(chunk, slot(chunk, 2, 0), base, RIGHT_FAR, ((PAIR_RIGHT_FAR, over, 1),), 1)
+            relay(chunk, slot(chunk, 3, 1), base, PAIR_LEFT, ())
+            relay(chunk, slot(chunk, 1, 1), base, PAIR_RIGHT, ())
+        else:
+            relay(chunk, slot(chunk, 3, 1), base, PAIR_LEFT, ((PAIR_LEFT_FAR, along(1), 0),))
+            relay(chunk, slot(chunk, 1, 1), base, PAIR_RIGHT, ((PAIR_RIGHT_FAR, along(3), 1),))
+            relay(chunk, slot(chunk, 2, 0), base, LEFT_FAR, (), 0)
+            relay(chunk, slot(chunk, 2, 0), base, RIGHT_FAR, (), 1)
 
     def third(plane, chunk):
         base, slot, along = plane
-        relay(chunk, slot(2, 1), base, PAIR_LEFT_FAR, (), 0)
-        relay(chunk, slot(2, 1), base, PAIR_RIGHT_FAR, (), 1)
+        relay(chunk, slot(chunk, 2, 1), base, PAIR_LEFT_FAR, (), 0)
+        relay(chunk, slot(chunk, 2, 1), base, PAIR_RIGHT_FAR, (), 1)
 
     row_first, column_first = functools.partial(first, planes[0]), functools.partial(first, planes[1])
     row_second, column_second = functools.partial(second, planes[0]), functools.partial(second, planes[1])
@@ -211,6 +208,8 @@
             arrived(chunk, row_slot(step, flip, 1 - c), CORE_BASE + event, half)
 
     def split(chunk):
+        own_column, place_x = column_slot(chunk, 0, 0), route(chunk)[10]
+
         @pl.loop(0, SHARDS)
         def _(shard):
             values = land[chunk, jnp.where(shard == own_column, place_x, shard)]
@@ -267,6 +266,7 @@
     turn_second(4)
     turn_third(2)
     turned(1)
+    begin(3)
     column_first(0)
     turn_second(5)
     turn_third(3)
@@ -276,12 +276,12 @@
 
     @pl.loop(0, chunks)
     def _(chunk):
+        ahead(chunk + 4, begin)
+        ahead(chunk + 4, turn_third)
+        ahead(chunk + 3, turned)
         ahead(chunk + 1, row_second)
         ahead(chunk + 2, row_first)
-        ahead(chunk + 3, begin)
         ahead(chunk + 6, turn_second)
-        ahead(chunk + 4, turn_third)
-        ahead(chunk + 3, turned)
         ahead(chunk + 1, column_second)
         ahead(chunk + 2, column_first)
         row_third(chunk)
@@ -289,50 +289,75 @@
         from_twin(chunk)
         split(chunk)
 
-        @pl.loop(0, perturbations)
-        def _(k):
-            multiply(k)
-
-            @pl.when(chunk == chunks - 1)
-            def _():
-                pltpu.make_async_copy(total.at[k], density_ref.at[k], out_sem.at[k]).start()
+        @pl.when(chunk < chunks - 1)
+        def _():
+            @pl.loop(0, perturbations)
+            def _(k):
+                multiply(k)
 
     @pl.loop(0, chunks)
     def _(chunk):
         sent = land.at[chunk, pl.ds(0, 22)]
         pltpu.make_async_copy(sent, sent, send_sem.at[chunk]).wait()
+        _, _, _, moved_z, goes_y, _, goes_x, _, _, _, _, _ = route(chunk)
         pl.when(moved_z)(lambda: turn_z(chunk).wait_send())
         pl.when(goes_y)(lambda: turn_y(chunk).wait_send())
         pl.when(goes_x)(lambda: turn_x(chunk).wait_send())
 
-    for k in range(perturbations):
-        pltpu.make_async_copy(total.at[k], density_ref.at[k], out_sem.at[k]).wait()
+
+def finish(high, low, total, density_ref):
+    k, m = pl.program_id(0), pl.program_id(1)
+    o = high.shape[0] - 1
+    height, width = density_ref.shape[1:]
+    ours = pl.ds(pl.multiple_of(m * height, height), height)
+    theirs = slice(high.shape[1] - width, high.shape[1])
+    left_side = jnp.concatenate(
+        [high[k, ours], high[k, ours], low[k, ours], high[o, ours], low[o, ours], high[o, ours]], axis=1
+    )
+    right_side = jnp.concatenate(
+        [high[o, theirs], low[o, theirs], high[o, theirs], high[k, theirs], high[k, theirs], low[k, theirs]], axis=1
+    )
+    density_ref[0] = total[k, ours] + lax.dot_general(
+        left_side, right_side, (((1,), (1,)), ((), ())), preferred_element_type=jnp.float32
+    )
 
 
 def shards(response_coeffs, occupied_coeffs):
     perturbations, rows, occupied = response_coeffs.shape
     depth = occupied // CHUNKS
-    return pl.pallas_call(
+    height, width = ROW_SHARDS * rows, COLUMN_SHARDS * rows
+    slices = (perturbations + 1, SHARDS * rows, depth)
+    high, low, total = pl.pallas_call(
         kernel,
         name="gather_multiply",
-        out_shape=jax.ShapeDtypeStruct((perturbations, ROW_SHARDS * rows, COLUMN_SHARDS * rows), jnp.float32),
-        in_specs=[pl.BlockSpec(memory_space=pl.ANY)] * 2,
-        out_specs=pl.BlockSpec(memory_space=pl.ANY),
+        out_shape=[
+            pltpu.VMEM(slices, jnp.bfloat16),
+            pltpu.VMEM(slices, jnp.bfloat16),
+            pltpu.VMEM((perturbations, height, width), jnp.float32),
+        ],
+        in_specs=[pl.BlockSpec(memory_space=pltpu.HBM)] * 2,
+        out_specs=[pl.BlockSpec(memory_space=pltpu.VMEM)] * 3,
         scratch_shapes=[
             pltpu.VMEM((CHUNKS, SHARDS + TURN_SLOTS, perturbations + 1, rows, depth), jnp.float32),
-            pltpu.VMEM((perturbations + 1, SHARDS * rows, depth), jnp.bfloat16),
-            pltpu.VMEM((perturbations + 1, SHARDS * rows, depth), jnp.bfloat16),
-            pltpu.VMEM((perturbations, ROW_SHARDS * rows, COLUMN_SHARDS * rows), jnp.float32),
             pltpu.SemaphoreType.DMA((CHUNKS, 2)),
             pltpu.SemaphoreType.DMA((CHUNKS,)),
             pltpu.SemaphoreType.DMA((CHUNKS, 3)),
             pltpu.SemaphoreType.DMA((CHUNKS, EVENTS)),
-            pltpu.SemaphoreType.DMA((perturbations,)),
         ],
         compiler_params=pltpu.CompilerParams(
-            collective_id=0, has_side_effects=True, vmem_limit_bytes=56 * 1024 * 1024
+            collective_id=0, has_side_effects=True, vmem_limit_bytes=57475072
         ),
     )(response_coeffs, occupied_coeffs)
+    tile = 1024
+    return pl.pallas_call(
+        finish,
+        name="finish",
+        grid=(perturbations, height // tile),
+        out_shape=jax.ShapeDtypeStruct((perturbations, height, width), jnp.float32),
+        in_specs=[pl.BlockSpec(memory_space=pltpu.VMEM)] * 3,
+        out_specs=pl.BlockSpec((1, tile, width), lambda k, m: (k, m, 0)),
+        compiler_params=pltpu.CompilerParams(vmem_limit_bytes=40 * 1024 * 1024),
+    )(high, low, total)
 
 
 def solution(mesh):

time: 119 us -> 110 us (0.924)
  local copies, waits for them, and re-layouts: 6.2 us -> 0 us
  Pallas kernels: 112 us -> 110 us
    unnamed x1 -> x0, local copies, waits for them, and re-layouts: 6.2 us -> none
    pallas_call x1 -> x2, Pallas kernels: 112 us -> 110 us  [the longest x1 105 us: shards(): pl.pallas_call(kernel, name='gather_multiply', out_shape=[pltpu.VMEM(slic...]
where the time goes in v3:
time: 110 us
  Pallas kernels  110 us (100%)
    pallas_call x1, Pallas kernels, shards(): pl.pallas_call(kernel, name='gather_multiply', out_shape=[pltpu.VMEM(slic...  105 us
    pallas_call x1, Pallas kernels, shards(): pl.pallas_call(finish, name='finish', grid=(perturbations, height // tile...  4.69 us

profile of v3, /device:TPU:1, one launch (start us, length us, event | category | flops | bytes accessed | tf_op | source)
XLA Modules:
  0.0 109.6 jit_solution(4281439461211541009)
XLA Ops:
  0.0 104.9 %gather_multiply.1 = (bf16[4,1536,128]{2,1,0:T(8,128)(2,1)S(1)}, bf16[4,1536,128]{2,1,0:T(8,128)(2,1)S(1)}, f32[3,1024,512]{2,1,0:T(8,128)S(1)}) custom-call(f32[3,64,1024]{2,1,0:T(8,128)} %response_ref.1, f32[64,1024]{1,0:T(8,128)} %occupied_ref.1), custom_call_target="tpu_custom_call" | custom-call | tf_op jit(solution)/shard_map/gather_multiply/pallas_call | solution.py:330
  104.9 4.7 %finish.1 = f32[3,1024,512]{2,1,0:T(8,128)} custom-call(bf16[4,1536,128]{2,1,0:T(8,128)(2,1)S(1)} %get-tuple-element.8.high, bf16[4,1536,128]{2,1,0:T(8,128)(2,1)S(1)} %get-tuple-element.9.low, f32[3,1024,512]{2,1,0:T(8,128)S(1)} %get-tuple-element.10.total), custom_call_target="tpu_custom_call" | custom-call | tf_op jit(solution)/shard_map/finish/pallas_call | solution.py:352

commit v4 on v3

--- a/solution.py
+++ b/solution.py
@@ -23,6 +23,7 @@
 CORE_OWN = 3 * PLANE_EVENTS
 TURN_BASE = CORE_OWN + 1
 EVENTS = TURN_BASE + 3
+CROSSED = {ROW_BASE: (4, ()), COLUMN_BASE: (4, (0, 2))}
 
 
 def kernel(response_ref, occupied_ref, high, low, total, land, load_sem, send_sem, turn_sem, recv_sem):
@@ -178,17 +179,21 @@
 
     def second(plane, chunk):
         base, slot, along = plane
-        if base in (COLUMN_BASE,):
-            over = across if base == COLUMN_BASE else near
-            relay(chunk, slot(chunk, 2, 0), base, LEFT_FAR, ((PAIR_LEFT_FAR, over, 0),), 0)
-            relay(chunk, slot(chunk, 2, 0), base, RIGHT_FAR, ((PAIR_RIGHT_FAR, over, 1),), 1)
-            relay(chunk, slot(chunk, 3, 1), base, PAIR_LEFT, ())
-            relay(chunk, slot(chunk, 1, 1), base, PAIR_RIGHT, ())
-        else:
-            relay(chunk, slot(chunk, 3, 1), base, PAIR_LEFT, ((PAIR_LEFT_FAR, along(1), 0),))
-            relay(chunk, slot(chunk, 1, 1), base, PAIR_RIGHT, ((PAIR_RIGHT_FAR, along(3), 1),))
-            relay(chunk, slot(chunk, 2, 0), base, LEFT_FAR, (), 0)
-            relay(chunk, slot(chunk, 2, 0), base, RIGHT_FAR, (), 1)
+        over = near if base == ROW_BASE else across
+        period, crossed_ones = CROSSED[base]
+        crossed = functools.reduce(jnp.logical_or, [chunk % period == one for one in crossed_ones], False)
+
+        def forward(when, slot_, event, peer, half):
+            pl.when(when)(lambda: send(chunk, slot_, slot_, base + event, peer, half))
+
+        relay(chunk, slot(chunk, 3, 1), base, PAIR_LEFT, ())
+        forward(jnp.logical_not(crossed), slot(chunk, 3, 1), PAIR_LEFT_FAR, along(1), 0)
+        relay(chunk, slot(chunk, 1, 1), base, PAIR_RIGHT, ())
+        forward(jnp.logical_not(crossed), slot(chunk, 1, 1), PAIR_RIGHT_FAR, along(3), 1)
+        relay(chunk, slot(chunk, 2, 0), base, LEFT_FAR, (), 0)
+        forward(crossed, slot(chunk, 2, 0), PAIR_LEFT_FAR, over, 0)
+        relay(chunk, slot(chunk, 2, 0), base, RIGHT_FAR, (), 1)
+        forward(crossed, slot(chunk, 2, 0), PAIR_RIGHT_FAR, over, 1)
 
     def third(plane, chunk):
         base, slot, along = plane
@@ -237,6 +242,10 @@
     def ahead(chunk, step):
         pl.when(chunk < chunks)(lambda: step(chunk))
 
+    @pl.loop(0, perturbations)
+    def _(k):
+        total[k] = jnp.zeros(total.shape[1:], jnp.float32)
+
     pl.semaphore_wait(barrier, len(peers))
     for chunk in range(3):
         turn_first(chunk)
@@ -247,30 +256,26 @@
         turn_first(chunk)
 
     turn_second(0)
+    begin(1)
     turn_second(1)
-    begin(1)
+    turn_third(0)
     turn_second(2)
-    turn_third(0)
     row_first(0)
+    turned(0)
+    turn_third(1)
+    begin(2)
+
     turn_second(3)
-    turn_third(1)
-    turned(0)
-    begin(2)
-
-    @pl.loop(0, perturbations)
-    def _(k):
-        total[k] = jnp.zeros(total.shape[1:], jnp.float32)
-
+    turn_third(2)
+    turned(1)
     row_second(0)
     row_first(1)
+    column_first(0)
     turn_second(4)
-    turn_third(2)
-    turned(1)
-    begin(3)
-    column_first(0)
-    turn_second(5)
     turn_third(3)
     turned(2)
+    begin(3)
+    turn_second(5)
     column_second(0)
     column_first(1)
 

time: 110 us -> 109 us (level)
  Pallas kernels: 110 us -> 108 us
where the time goes in v4:
time: 109 us
  Pallas kernels  108 us (99%)
    pallas_call x1, Pallas kernels, shards(): pl.pallas_call(kernel, name='gather_multiply', out_shape=[pltpu.VMEM(slic...  104 us
    pallas_call x1, Pallas kernels, shards(): pl.pallas_call(finish, name='finish', grid=(perturbations, height // tile...  4.68 us

profile of v4, /device:TPU:1, one launch (start us, length us, event | category | flops | bytes accessed | tf_op | source)
XLA Modules:
  0.0 108.5 jit_solution(14834133077448141170)
XLA Ops:
  0.0 103.8 %gather_multiply.1 = (bf16[4,1536,128]{2,1,0:T(8,128)(2,1)S(1)}, bf16[4,1536,128]{2,1,0:T(8,128)(2,1)S(1)}, f32[3,1024,512]{2,1,0:T(8,128)S(1)}) custom-call(f32[3,64,1024]{2,1,0:T(8,128)} %response_ref.1, f32[64,1024]{1,0:T(8,128)} %occupied_ref.1), custom_call_target="tpu_custom_call" | custom-call | tf_op jit(solution)/shard_map/gather_multiply/pallas_call | solution.py:335
  103.8 4.7 %finish.1 = f32[3,1024,512]{2,1,0:T(8,128)} custom-call(bf16[4,1536,128]{2,1,0:T(8,128)(2,1)S(1)} %get-tuple-element.8.high, bf16[4,1536,128]{2,1,0:T(8,128)(2,1)S(1)} %get-tuple-element.9.low, f32[3,1024,512]{2,1,0:T(8,128)S(1)} %get-tuple-element.10.total), custom_call_target="tpu_custom_call" | custom-call | tf_op jit(solution)/shard_map/finish/pallas_call | solution.py:357

commit v5 on v4

--- a/solution.py
+++ b/solution.py
@@ -286,19 +286,16 @@
         ahead(chunk + 3, turned)
         ahead(chunk + 1, row_second)
         ahead(chunk + 2, row_first)
+        pl.when(chunk > 0)(lambda: multiply(0))
         ahead(chunk + 6, turn_second)
         ahead(chunk + 1, column_second)
         ahead(chunk + 2, column_first)
+        pl.when(chunk > 0)(lambda: multiply(1))
         row_third(chunk)
+        pl.when(chunk > 0)(lambda: multiply(2))
         column_third(chunk)
         from_twin(chunk)
         split(chunk)
-
-        @pl.when(chunk < chunks - 1)
-        def _():
-            @pl.loop(0, perturbations)
-            def _(k):
-                multiply(k)
 
     @pl.loop(0, chunks)
     def _(chunk):

time: 109 us -> 109 us (level); the launches traced: 109 us -> 107 us
    pallas_call x1, Pallas kernels: 104 us -> 103 us  [shards(): pl.pallas_call(kernel, name='gather_multiply', out_shape=[pltpu.VMEM(slic...]
where the time goes in v5:
time: 109 us; the launch traced here: 107 us
  Pallas kernels  107 us (98%)
    pallas_call x1, Pallas kernels, shards(): pl.pallas_call(kernel, name='gather_multiply', out_shape=[pltpu.VMEM(slic...  103 us
    pallas_call x1, Pallas kernels, shards(): pl.pallas_call(finish, name='finish', grid=(perturbations, height // tile...  4.68 us

profile of v5, /device:TPU:1, one launch (start us, length us, event | category | flops | bytes accessed | tf_op | source)
XLA Modules:
  0.0 107.2 jit_solution(1688598159689826263)
XLA Ops:
  0.0 102.5 %gather_multiply.1 = (bf16[4,1536,128]{2,1,0:T(8,128)(2,1)S(1)}, bf16[4,1536,128]{2,1,0:T(8,128)(2,1)S(1)}, f32[3,1024,512]{2,1,0:T(8,128)S(1)}) custom-call(f32[3,64,1024]{2,1,0:T(8,128)} %response_ref.1, f32[64,1024]{1,0:T(8,128)} %occupied_ref.1), custom_call_target="tpu_custom_call" | custom-call | tf_op jit(solution)/shard_map/gather_multiply/pallas_call | solution.py:332
  102.6 4.7 %finish.1 = f32[3,1024,512]{2,1,0:T(8,128)} custom-call(bf16[4,1536,128]{2,1,0:T(8,128)(2,1)S(1)} %get-tuple-element.8.high, bf16[4,1536,128]{2,1,0:T(8,128)(2,1)S(1)} %get-tuple-element.9.low, f32[3,1024,512]{2,1,0:T(8,128)S(1)} %get-tuple-element.10.total), custom_call_target="tpu_custom_call" | custom-call | tf_op jit(solution)/shard_map/finish/pallas_call | solution.py:354
